TPU v7x, 32 devices: a whole 2x2x4 slice. The times are simulated.
32 devices in a mesh: grp: 4 (over y, x), sub: 8 (over z, core).
Axes of the slice: x: 2, y: 2, z: 4, core: 2. Of those that a mesh axis runs over, the one named last changes fastest.
Arguments:
- bem_tiles: float32 [4096, 4096], P('grp', 'sub'), may hold values from -0.0625 to 0.0625
- leaf_inverse: float32 [4, 16, 1024, 1024], P('grp', 'sub'), may hold values from -1.5 to 1.5
- coupling: float32 [4, 16, 1024, 512], P('grp', 'sub'), may hold values from -0.0625 to 0.0625
- schur_inverse: float32 [4, 512, 512], P('grp', None, 'sub'), may hold values from -1.5 to 1.5
- leaf_load: float32 [4, 16, 1024, 128], P('grp', 'sub'), may hold values from -6 to 6
- sep_load: float32 [4, 512, 128], P('grp'), may hold values from -6 to 6
- surf_load: float32 [4096, 128], P(('grp', 'sub')), may hold values from -6 to 6
- surf_start: float32 [4096, 128], P(('grp', 'sub')), may hold values from -6 to 6
- flux_weight: float32 [4, 16, 8, 128], P('grp', 'sub'), may hold values from 0.25 to 1
- trace_weight: float32 [4, 16, 8, 128], P('grp', 'sub'), may hold values from 0.25 to 1
- leaf_sizes: int32 [4, 16], P('grp', 'sub'), may hold values from 512 to 1024
- block_counts: int32 [4, 16], P('grp', 'sub'), may hold values from 4 to 8
- block_owner: int32 [4, 16, 8, 1], P('grp', 'sub'), may hold values from 0 to 7; in each aligned block of 16 rows (0 to 15, 16 to 31, ..., all dimensions but the last counted through in order) at most 2 rows name the same one
Outputs:
- solution: float32 [4, 16, 1024, 128], P('grp', 'sub')
- sep_value: float32 [4, 512, 128], P('grp', 'sub')
- pressure: float32 [4096, 128], P(('grp', 'sub'))
Inputs may be any that keep to these rules, and one draw needn't show every extreme that they name: `block_owner`: of the 16 entries of one device, live or not, at most 2 name the same owner, and some device has 2 entries naming one owner.
All inputs are finite; a program needn't handle non-finite values.
Results may differ from a plain program's by a relative error of at most 0.00018.
Values sent between devices are 32-bit elements; how exact they have to be, the bound alone decides.
A program may use at most 128 MiB of HBM per device.

v0:
```python
import jax
import jax.numpy as jnp
from jax import lax
from jax.sharding import PartitionSpec as P

CAP = 2
SWEEPS = 3


def on_device(
    bem_tiles,
    leaf_inverse,
    coupling,
    schur_inverse,
    leaf_load,
    sep_load,
    surf_load,
    surf_start,
    flux_weight,
    trace_weight,
    leaf_sizes,
    block_counts,
    block_owner,
):
    highest = lax.Precision.HIGHEST
    parts = lax.axis_size("sub")
    here = lax.axis_index("sub")
    width = surf_load.shape[0]
    loads = surf_load.shape[1]
    leaves = leaf_inverse.shape[1]
    order = leaf_inverse.shape[2]
    blocks = order // width
    entries = leaves * blocks
    separator = schur_inverse.shape[1]
    sep_share = schur_inverse.shape[2]
    row_mask = (jnp.arange(order, dtype=jnp.int32)[None, :] < leaf_sizes[0][:, None]).astype(
        jnp.float32
    )[:, :, None]
    active = (
        (jnp.arange(blocks, dtype=jnp.int32)[None, :] < block_counts[0][:, None])
        .astype(jnp.float32)
        .reshape(entries)
    )
    owner = block_owner[0, :, :, 0].reshape(entries)
    picker = (owner[:, None] == jnp.arange(parts, dtype=jnp.int32)[None, :]).astype(jnp.float32)
    live_pick = picker * active[:, None]
    flux_scale = flux_weight[0].reshape(entries, width)[:, :, None]
    trace_scale = (trace_weight[0].reshape(entries, width) * active[:, None])[:, :, None]
    position = jnp.arange(entries, dtype=jnp.int32)
    earlier = (position[:, None] > position[None, :]) & (owner[:, None] == owner[None, :])
    slot_index = jnp.sum(earlier.astype(jnp.int32), axis=1)
    target = owner * CAP + slot_index
    placing = (jnp.arange(parts * CAP, dtype=jnp.int32)[:, None] == target[None, :]).astype(
        jnp.float32
    )
    schur_full = lax.all_gather(schur_inverse[0], "sub", axis=1, tiled=True)
    pressure = surf_start
    sep_value = jnp.zeros((separator, loads), jnp.float32)
    solution = jnp.zeros((leaves, order, loads), jnp.float32)
    for sweep in range(SWEEPS):
        column = lax.all_gather(pressure, "grp", axis=0, tiled=True)

        def tile_product(start, count, column=column):
            return jnp.dot(bem_tiles, column, precision=highest, preferred_element_type=jnp.float32)

        applied = lax.psum_scatter(
            tile_product(jnp.int32(0), lax.axis_size("sub") * width),
            "sub",
            scatter_dimension=0,
            tiled=True,
        )
        surface_patch = lax.all_gather(pressure, "sub", axis=0, tiled=True).reshape(
            parts, width, loads
        )
        flux = jnp.einsum("eo,oil->eil", live_pick, surface_patch, precision=highest) * flux_scale
        flux = flux.reshape(leaves, order, loads)
        pulled = jnp.einsum("jrs,sl->jrl", coupling[0], sep_value, precision=highest)
        rhs = (leaf_load[0] - pulled - flux) * row_mask
        solution = jnp.einsum("jrc,jcl->jrl", leaf_inverse[0], rhs, precision=highest) * row_mask
        partial_sum = jnp.einsum("jrs,jrl->sl", coupling[0], solution, precision=highest)
        summed = lax.psum(partial_sum, "sub")
        sep_value = jnp.dot(
            schur_full, sep_load[0] - summed, precision=highest, preferred_element_type=jnp.float32
        )
        weighted = solution.reshape(entries, width, loads) * trace_scale
        outgoing = jnp.dot(
            placing,
            weighted.reshape(entries, width * loads),
            precision=highest,
            preferred_element_type=jnp.float32,
        )
        incoming = lax.all_to_all(
            outgoing.reshape(parts, CAP, width, loads),
            "sub",
            split_axis=0,
            concat_axis=0,
            tiled=True,
        )
        trace = jnp.sum(incoming, axis=(0, 1))
        pressure = surf_load + applied + trace
    sep_rows_out = lax.dynamic_slice_in_dim(sep_value, here * sep_share, sep_share, 0)
    return (solution[None], sep_rows_out[None], pressure)


def solution(mesh):
    return jax.shard_map(
        on_device,
        mesh=mesh,
        in_specs=(
            P("grp", "sub"),
            P("grp", "sub", None, None),
            P("grp", "sub", None, None),
            P("grp", None, "sub"),
            P("grp", "sub", None, None),
            P("grp", None, None),
            P(("grp", "sub"), None),
            P(("grp", "sub"), None),
            P("grp", "sub", None, None),
            P("grp", "sub", None, None),
            P("grp", "sub"),
            P("grp", "sub"),
            P("grp", "sub", None, None),
        ),
        out_specs=(P("grp", "sub", None, None), P("grp", "sub", None), P(("grp", "sub"), None)),
        check_vma=False,
    )
```

profile of v0, /device:TPU:0, one launch (start us, length us, event | category | flops | bytes accessed | tf_op | source)
XLA Modules:
  0.0 464.7 jit_solution(11380869395240890339)
XLA Ops:
  7.3 10.9 %all_gather.23 = f32[512,128]{1,0:T(8,128)S(1)} all-gather(f32[128,128]{1,0:T(8,128)} %param.20), channel_id=1, replica_groups=mesh['grp'=4,'sub'=8] {'grp'}, dimensions={0}, use_global_device_ids=true | all-gather | bytes 327680 | tf_op jit(solution)/shard_map/all_gather | solution.py:61
  18.2 2.6 fusion.127
  20.8 15.6 %all_gather.21 = f32[1024,128]{1,0:T(8,128)S(1)} all-gather(f32[128,128]{1,0:T(8,128)} %param.20), channel_id=1, replica_groups=mesh['grp'=4,'sub'=8] {'sub'}, dimensions={0}, use_global_device_ids=true | all-gather | bytes 589824 | tf_op jit(solution)/shard_map/all_gather | solution.py:72
  39.7 1.3 copy.80
  41.0 1.6 copy.75
  42.6 7.2 %fusion.51 = f32[2,1024,128]{1,2,0:T(8,128)S(1)} fusion(f32[2,1024,128]{1,2,0:T(8,128)} %copy.80, f32[1,2,1024,512]{3,2,1,0:T(8,128)} %param.15, f32[1,2,1024,128]{2,3,1,0:T(8,128)S(1)} %copy.75, f32[2,1024]{1,0:T(2,128)S(1)} %compare_convert_fusion), kind=kOutput, calls=%fused_computation.29 | convolution fusion | flops 1611399168 | bytes 7348224 | tf_op jit(solution)/shard_map/jrs,sl->jrl/dot_general | solution.py:77
  49.8 12.1 %fusion.57 = f32[2,1024,128]{1,2,0:T(8,128)} fusion(f32[2,1024,128]{1,2,0:T(8,128)S(1)} %fusion.51, f32[1,2,1024,1024]{3,2,1,0:T(8,128)} %param.14, f32[2,1024]{1,0:T(2,128)S(1)} %compare_convert_fusion), kind=kOutput, calls=%fused_computation.34 | convolution fusion | flops 3221487616 | bytes 10493952 | tf_op jit(solution)/shard_map/jrc,jcl->jrl/dot_general | solution.py:79
  62.0 1.6 copy.81
  65.0 2.4 fusion.85
  68.7 5.2 %all-to-all-start = ((f32[8,2,128,128]{3,2,1,0:T(8,128)}), f32[8,2,128,128]{3,2,1,0:T(8,128)}, u32[]{:S(2)}, u32[]{:S(2)}) async-start(f32[8,2,128,128]{3,2,1,0:T(8,128)} %copy.83), calls=%async_computation.1 | async-start | bytes 2097152 | tf_op jit(solution)/shard_map/all_to_all | solution.py:92
  74.3 5.7 %fusion.69 = f32[512,128]{0,1:T(8,128)} fusion(f32[2,1024,128]{1,2,0:T(8,128)} %fusion.57, f32[1,2,1024,512]{3,2,1,0:T(8,128)} %param.15), kind=kOutput, calls=%fused_computation.40 | convolution fusion | flops 1610612736 | bytes 5505024 | tf_op jit(solution)/shard_map/jrs,jrl->sl/dot_general | solution.py:80
  81.8 20.1 %all-to-all-done = f32[8,2,128,128]{3,2,1,0:T(8,128)} async-done(((f32[8,2,128,128]{3,2,1,0:T(8,128)}), f32[8,2,128,128]{3,2,1,0:T(8,128)}, u32[]{:S(2)}, u32[]{:S(2)}) %all-to-all-start) | async-done | bytes 1048608 | tf_op jit(solution)/shard_map/all_to_all | solution.py:92
  101.9 1.9 reduce_sum.37
  104.8 14.8 %all_gather.24 = f32[1024,128]{1,0:T(8,128)S(1)} all-gather(f32[128,128]{1,0:T(8,128)S(1)} %add_add_fusion.2), channel_id=1, replica_groups=mesh['grp'=4,'sub'=8] {'sub'}, dimensions={0}, use_global_device_ids=true | all-gather | bytes 589824 | tf_op jit(solution)/shard_map/all_gather | solution.py:72
  119.5 1.8 convolution_multiply_fusion.1
  122.7 2.6 copy.86
  125.2 15.9 %all-reduce.4.cloned.1.call-done = f32[512,128]{0,1:T(8,128)} async-done(((f32[512,128]{0,1:T(8,128)}), f32[512,128]{0,1:T(8,128)}) %all-reduce.4.cloned.1.call-update) | async-done | bytes 262160 | tf_op jit(solution)/shard_map/psum | solution.py:81
  141.2 22.9 %all-gather.3.cloned.1.call-done = f32[1,512,512]{1,2,0:T(8,128)} async-done(((f32[1,512,64]{1,2,0:T(8,128)}), f32[1,512,512]{1,2,0:T(8,128)}) %all-gather.3.cloned.1.call-update) | async-done | bytes 1048592 | tf_op jit(solution)/shard_map/all_gather | solution.py:56
  164.1 2.0 convolution_bitcast_fusion.3
  166.1 7.2 %fusion.42 = f32[2,1024,128]{1,2,0:T(8,128)S(1)} fusion(f32[2,1024,128]{1,2,0:T(8,128)} %copy.86, f32[128,512,1]{1,0,2:T(8,128)S(1)} %convolution_bitcast_fusion.3, f32[1,2,1024,512]{3,2,1,0:T(8,128)} %param.15, f32[1,2,1024,128]{2,3,1,0:T(8,128)} %copy-done.2, f32[2,1024]{1,0:T(2,128)S(1)} %compare_convert_fusion), kind=kOutput, calls=%fused_computation.26 | convolution fusion | flops 1611399168 | bytes 7610368 | tf_op jit(solution)/shard_map/jrs,sl->jrl/dot_general | solution.py:77
  173.3 12.1 %fusion.63 = f32[2,1024,128]{1,2,0:T(8,128)} fusion(f32[2,1024,128]{1,2,0:T(8,128)S(1)} %fusion.42, f32[1,2,1024,1024]{3,2,1,0:T(8,128)} %param.14, f32[2,1024]{1,0:T(2,128)S(1)} %compare_convert_fusion), kind=kOutput, calls=%fused_computation.36 | convolution fusion | flops 3221487616 | bytes 10493952 | tf_op jit(solution)/shard_map/jrc,jcl->jrl/dot_general | solution.py:79
  185.4 2.6 copy.88
  188.0 2.4 reshape.166
  190.4 2.5 fusion.83
  194.0 4.2 all-to-all-start.1
  198.5 5.7 %fusion.72 = f32[512,128]{0,1:T(8,128)} fusion(f32[2,1024,128]{1,2,0:T(8,128)} %fusion.63, f32[1,2,1024,512]{3,2,1,0:T(8,128)} %param.15), kind=kOutput, calls=%fused_computation.41 | convolution fusion | flops 1610612736 | bytes 5505024 | tf_op jit(solution)/shard_map/jrs,jrl->sl/dot_general | solution.py:80
  204.2 9.0 %all_gather.25 = f32[512,128]{1,0:T(8,128)S(1)} all-gather(f32[128,128]{1,0:T(8,128)S(1)} %add_add_fusion.2), channel_id=1, replica_groups=mesh['grp'=4,'sub'=8] {'grp'}, dimensions={0}, use_global_device_ids=true | all-gather | bytes 327680 | tf_op jit(solution)/shard_map/all_gather | solution.py:61
  213.2 3.1 convolution_bitcast_fusion.1
  216.3 1.6 copy.87
  217.9 48.1 %all-reduce.6.cloned.1.call-done = f32[512,128]{0,1:T(8,128)} async-done(((f32[512,128]{0,1:T(8,128)}), f32[512,128]{0,1:T(8,128)}) %all-reduce.6.cloned.1.call-update) | async-done | bytes 262160 | tf_op jit(solution)/shard_map/psum | solution.py:81
  266.0 2.7 convolution_bitcast_fusion.2
  270.8 28.2 %reduce-scatter.6.cloned.1.call-done = f32[128,128]{0,1:T(8,128)} async-done(((f32[1024,128]{0,1:T(8,128)}), f32[128,128]{0,1:T(8,128)}) %reduce-scatter.6.cloned.1.call-update) | async-done | bytes 65552 | tf_op jit(solution)/shard_map/reduce_scatter | solution.py:66
  299.9 14.9 %all_gather.26 = f32[1024,128]{0,1:T(8,128)S(1)} all-gather(f32[128,128]{0,1:T(8,128)S(1)} %add_add_fusion.1), channel_id=1, replica_groups=mesh['grp'=4,'sub'=8] {'sub'}, dimensions={0}, use_global_device_ids=true | all-gather | bytes 589824 | tf_op jit(solution)/shard_map/all_gather | solution.py:72
  315.7 2.0 copy.93
  317.8 2.1 convolution_multiply_fusion
  321.1 2.6 copy.95
  323.7 7.2 %fusion.33 = f32[2,1024,128]{1,2,0:T(8,128)S(1)} fusion(f32[2,1024,128]{1,2,0:T(8,128)} %copy.95, f32[128,512,1]{1,0,2:T(8,128)} %convolution_bitcast_fusion.2, f32[1,2,1024,512]{3,2,1,0:T(8,128)} %param.15, f32[1,2,1024,128]{2,3,1,0:T(8,128)} %copy-done.2, f32[2,1024]{1,0:T(2,128)S(1)} %compare_convert_fusion), kind=kOutput, calls=%fused_computation.23 | convolution fusion | flops 1611399168 | bytes 7610368 | tf_op jit(solution)/shard_map/jrs,sl->jrl/dot_general | solution.py:77
  330.9 12.1 %fusion.66 = f32[2,128,1024]{2,1,0:T(8,128)} fusion(f32[2,1024,128]{1,2,0:T(8,128)S(1)} %fusion.33, f32[1,2,1024,1024]{3,2,1,0:T(8,128)} %param.14, f32[2,1024]{1,0:T(2,128)S(1)} %compare_convert_fusion), kind=kOutput, calls=%fused_computation.37 | convolution fusion | flops 3221487616 | bytes 10493952 | tf_op jit(solution)/shard_map/jrc,jcl->jrl/dot_general | solution.py:79
  343.0 2.6 copy.97
  345.7 2.4 reshape.169
  348.1 2.4 fusion.81
  351.7 4.2 all-to-all-start.2
  356.2 5.3 %fusion.75 = f32[512,128]{0,1:T(8,128)} fusion(f32[1,2,1024,512]{3,2,1,0:T(8,128)} %param.15, f32[2,128,1024]{2,1,0:T(8,128)S(1)} %copy-done.1), kind=kOutput, calls=%fused_computation.42 | convolution fusion | flops 1610612736 | bytes 5505024 | tf_op jit(solution)/shard_map/jrs,jrl->sl/dot_general | solution.py:80
  361.6 10.3 %all_gather.27 = f32[512,128]{0,1:T(8,128)S(1)} all-gather(f32[128,128]{0,1:T(8,128)S(1)} %add_add_fusion.1), channel_id=1, replica_groups=mesh['grp'=4,'sub'=8] {'grp'}, dimensions={0}, use_global_device_ids=true | all-gather | bytes 327680 | tf_op jit(solution)/shard_map/all_gather | solution.py:61
  371.9 3.1 convolution_bitcast_fusion
  376.3 47.2 %all-reduce.8.cloned.1.call-done = f32[512,128]{0,1:T(8,128)} async-done(((f32[512,128]{0,1:T(8,128)}), f32[512,128]{0,1:T(8,128)}) %all-reduce.8.cloned.1.call-update) | async-done | bytes 262160 | tf_op jit(solution)/shard_map/psum | solution.py:81
  423.6 3.1 fusion.87
  428.7 27.4 %reduce-scatter.8.cloned.1.call-done = f32[128,128]{0,1:T(8,128)} async-done(((f32[1024,128]{0,1:T(8,128)}), f32[128,128]{0,1:T(8,128)}) %reduce-scatter.8.cloned.1.call-update) | async-done | bytes 65552 | tf_op jit(solution)/shard_map/reduce_scatter | solution.py:66
  (73 shorter events, 23.6 us)
Async XLA Ops:
  7.2 11.0 %copy-start = (f32[1024,512]{1,0:T(8,128)S(1)}, f32[1024,512]{1,0:T(8,128)}, u32[]{:S(2)}) copy-start(f32[1024,512]{1,0:T(8,128)} %param.13) | copy-start | bytes 6291460
  7.2 29.7 %copy-start.9 = (s32[1,2,8,1]{2,3,1,0:T(1,128)S(1)}, s32[1,2,8,1]{2,3,1,0:T(1,128)}, u32[]{:S(2)}) copy-start(s32[1,2,8,1]{2,3,1,0:T(1,128)} %param.25) | copy-start | bytes 196
  7.2 30.6 %copy-start.11 = (s32[1,2]{1,0:T(1,128)S(1)}, s32[1,2]{1,0:T(1,128)}, u32[]{:S(2)}) copy-start(s32[1,2]{1,0:T(1,128)} %param.24) | copy-start | bytes 28
  7.2 30.8 %copy-start.10 = (s32[1,2]{1,0:T(1,128)S(1)}, s32[1,2]{1,0:T(1,128)}, u32[]{:S(2)}) copy-start(s32[1,2]{1,0:T(1,128)} %param.23) | copy-start | bytes 28
  7.2 30.8 %copy-start.4 = (f32[1,2,8,128]{3,2,1,0:T(8,128)S(1)}, f32[1,2,8,128]{3,2,1,0:T(8,128)}, u32[]{:S(2)}) copy-start(f32[1,2,8,128]{3,2,1,0:T(8,128)} %param.21) | copy-start | bytes 24580
  7.2 30.9 %copy-start.5 = (f32[1,2,8,128]{3,2,1,0:T(8,128)S(1)}, f32[1,2,8,128]{3,2,1,0:T(8,128)}, u32[]{:S(2)}) copy-start(f32[1,2,8,128]{3,2,1,0:T(8,128)} %param.22) | copy-start | bytes 24580
  7.2 96.6 %reduce-scatter.4.cloned.1.call-start = ((), (), s32[]{:S(2)}) async-start(), calls=%async_computation.7 | async-start | bytes 589824 | tf_op jit(solution)/shard_map/reduce_scatter | solution.py:66
  37.6 24.3 %copy-start.6 = (s32[16]{0:T(128)}, s32[16]{0:T(128)S(1)}, u32[]{:S(2)}) copy-start(s32[16]{0:T(128)S(1)} %eq.58) | copy-start | bytes 196
  42.6 19.3 %copy-start.2 = (f32[1,2,1024,128]{2,3,1,0:T(8,128)}, f32[1,2,1024,128]{2,3,1,0:T(8,128)S(1)}, u32[]{:S(2)}) copy-start(f32[1,2,1024,128]{2,3,1,0:T(8,128)S(1)} %copy.75) | copy-start | bytes 3145732
  61.9 5.5 %copy-start.7 = (s32[16]{0:T(128)}, s32[16]{0:T(128)S(1)}, u32[]{:S(2)}) copy-start(s32[16]{0:T(128)S(1)} %multiply_add_fusion.1) | copy-start | bytes 196
  68.7 33.3 %all-to-all-start = ((f32[8,2,128,128]{3,2,1,0:T(8,128)}), f32[8,2,128,128]{3,2,1,0:T(8,128)}, u32[]{:S(2)}, u32[]{:S(2)}) async-start(f32[8,2,128,128]{3,2,1,0:T(8,128)} %copy.83), calls=%async_computation.1 | async-start | bytes 2097152 | tf_op jit(solution)/shard_map/all_to_all | solution.py:92
  73.8 67.3 %all-reduce.4.cloned.1.call-start = ((), (), s32[]{:S(2)}) async-start(), calls=%async_computation.6 | async-start | bytes 524288 | tf_op jit(solution)/shard_map/psum | solution.py:81
  80.0 84.1 %all-gather.3.cloned.1.call-start = ((), (), s32[]{:S(2)}) async-start(), calls=%async_computation.12 | async-start | bytes 1179648 | tf_op jit(solution)/shard_map/all_gather | solution.py:56
  194.0 74.8 %all-to-all-start.1 = ((f32[8,2,128,128]{3,2,1,0:T(8,128)}), f32[8,2,128,128]{3,2,1,0:T(8,128)}, u32[]{:S(2)}, u32[]{:S(2)}) async-start(f32[8,2,128,128]{3,2,1,0:T(8,128)} %copy.90), calls=%async_computation.3 | async-start | bytes 2097152 | tf_op jit(solution)/shard_map/all_to_all | solution.py:92
  198.3 67.8 %all-reduce.6.cloned.1.call-start = ((), (), s32[]{:S(2)}) async-start(), calls=%async_computation.8 | async-start | bytes 524288 | tf_op jit(solution)/shard_map/psum | solution.py:81
  204.2 94.8 %reduce-scatter.6.cloned.1.call-start = ((), (), s32[]{:S(2)}) async-start(), calls=%async_computation.9 | async-start | bytes 589824 | tf_op jit(solution)/shard_map/reduce_scatter | solution.py:66
  343.0 5.0 %copy-start.8 = (s32[16]{0:T(128)S(1)}, s32[16]{0:T(128)}, u32[]{:S(2)}) copy-start(s32[16]{0:T(128)} %copy-done.7) | copy-start | bytes 196
  350.5 5.7 %copy-start.1 = (f32[2,128,1024]{2,1,0:T(8,128)S(1)}, f32[2,128,1024]{2,1,0:T(8,128)}, u32[]{:S(2)}) copy-start(f32[2,128,1024]{2,1,0:T(8,128)} %fusion.66) | copy-start | bytes 3145732
  351.7 75.6 %all-to-all-start.2 = ((f32[8,2,128,128]{3,2,1,0:T(8,128)}), f32[8,2,128,128]{3,2,1,0:T(8,128)}, u32[]{:S(2)}, u32[]{:S(2)}) async-start(f32[8,2,128,128]{3,2,1,0:T(8,128)} %copy.99), calls=%async_computation.5 | async-start | bytes 2097152 | tf_op jit(solution)/shard_map/all_to_all | solution.py:92
  356.0 67.6 %all-reduce.8.cloned.1.call-start = ((), (), s32[]{:S(2)}) async-start(), calls=%async_computation.10 | async-start | bytes 524288 | tf_op jit(solution)/shard_map/psum | solution.py:81
  361.6 94.5 %reduce-scatter.8.cloned.1.call-start = ((), (), s32[]{:S(2)}) async-start(), calls=%async_computation.11 | async-start | bytes 589824 | tf_op jit(solution)/shard_map/reduce_scatter | solution.py:66
  371.9 84.2 %copy-start.3 = (f32[128,128]{0,1:T(8,128)S(1)}, f32[128,128]{0,1:T(8,128)}, u32[]{:S(2)}) copy-start(f32[128,128]{0,1:T(8,128)} %copy.87) | copy-start | bytes 196612
Sparse Core Ops, SparseCore 0:
  20.9 31.6 reduce-scatter.3
  80.1 61.0 all-reduce.3
  142.8 21.2 all-gather.2
  204.3 61.7 all-reduce.5
  268.7 30.1 reduce-scatter.5
  361.7 61.8 all-reduce.7
  425.8 30.1 reduce-scatter.7
where the time goes:
time: 468 us; the launch traced here: 465 us
  waiting for transfers between devices  211 us (45%)
  matrix products  104 us (22%)
  blocking collectives  75.4 us (16%)
  local copies, waits for them, and re-layouts  37.4 us (8%)
  starting transfers between devices  14.7 us (3%)
  between operations  14.6 us (3%)
  other arithmetic  8.24 us (2%)
    psum x3, waiting for transfers between devices, on_device(): summed = lax.psum(partial_sum, 'sub')  111 us
    reduce_scatter x3, waiting for transfers between devices, on_device(): lax.psum_scatter(tile_product(jnp.int32(0), lax.axis_size('sub') * width)...  55.5 us
    all_gather x3, blocking collectives, on_device(): lax.all_gather(pressure, 'sub', axis=0, tiled=True)  45.3 us
    dot_general x3, matrix products, on_device(): jnp.einsum('jrc,jcl->jrl', leaf_inverse[0], rhs, precision=highest)  36.3 us
    all_gather x3, blocking collectives, on_device(): column = lax.all_gather(pressure, 'grp', axis=0, tiled=True)  30.1 us
    all_gather x1, waiting for transfers between devices, on_device(): schur_full = lax.all_gather(schur_inverse[0], 'sub', axis=1, tiled=True)  22.9 us
    dot_general x3, matrix products, on_device(): jnp.einsum('jrs,sl->jrl', coupling[0], sep_value, precision=highest)  21.6 us
    all_to_all x3, waiting for transfers between devices, on_device(): lax.all_to_all(outgoing.reshape(parts, CAP, width, loads), 'sub', split_a...  20.1 us
  transfers between devices with their start and end apart: 10, of which 7 were waited for; matrix products, arithmetic and copies ran while one was open for 17% of the time, Pallas kernels for 0%

commit v1 on v0

--- a/solution.py
+++ b/solution.py
@@ -78,7 +78,9 @@
         rhs = (leaf_load[0] - pulled - flux) * row_mask
         solution = jnp.einsum("jrc,jcl->jrl", leaf_inverse[0], rhs, precision=highest) * row_mask
         partial_sum = jnp.einsum("jrs,jrl->sl", coupling[0], solution, precision=highest)
-        summed = lax.psum(partial_sum, "sub")
+        summed = partial_sum
+        for hop in (1, 2, 4):
+            summed = summed + lax.ppermute(summed, "sub", [(dev, dev ^ hop) for dev in range(8)])
         sep_value = jnp.dot(
             schur_full, sep_load[0] - summed, precision=highest, preferred_element_type=jnp.float32
         )

time: 468 us -> 353 us (0.75)
  waiting for transfers between devices: 211 us -> 76.7 us
  starting transfers between devices: 14.7 us -> 26.9 us
  other arithmetic: 8.24 us -> 13.3 us
    psum x3 -> x0, waiting for transfers between devices: 111 us -> none  [on_device(): summed = lax.psum(partial_sum, 'sub')]
    ppermute x0 -> x9, waiting for transfers between devices: none -> 76.3 us  [on_device(): lax.ppermute(summed, 'sub', [(dev, dev ^ hop) for dev in range(8)])]
    reduce_scatter x3, waiting for transfers between devices: 55.5 us -> 0.02 us  [on_device(): lax.psum_scatter(tile_product(jnp.int32(0), lax.axis_size('sub') * width)...]
    all_gather x1, waiting for transfers between devices: 22.9 us -> 0.01 us  [on_device(): schur_full = lax.all_gather(schur_inverse[0], 'sub', axis=1, tiled=True)]
    all_to_all x3, waiting for transfers between devices: 20.1 us -> 0.01 us  [on_device(): lax.all_to_all(outgoing.reshape(parts, CAP, width, loads), 'sub', split_a...]
    ppermute x0 -> x9, starting transfers between devices: none -> 12.3 us  [on_device(): lax.ppermute(summed, 'sub', [(dev, dev ^ hop) for dev in range(8)])]
    add x0 -> x6, other arithmetic: none -> 5.1 us  [on_device(): summed + lax.ppermute(summed, 'sub', [(dev, dev ^ hop) for dev in range(8)])]
  transfers between devices with their start and end apart: 10 -> 16, of which waited for: 7 -> 7; matrix products, arithmetic and copies ran while one was open for 17% -> 23% of each run, Pallas kernels for 0% -> 0%
where the time goes in v1:
time: 353 us; the launch traced here: 349 us
  matrix products  102 us (29%)
  blocking collectives  78.9 us (22%)
  waiting for transfers between devices  76.7 us (22%)
  local copies, waits for them, and re-layouts  36.4 us (10%)
  starting transfers between devices  26.9 us (8%)
  between operations  14.3 us (4%)
  other arithmetic  13.3 us (4%)
    ppermute x9, waiting for transfers between devices, on_device(): lax.ppermute(summed, 'sub', [(dev, dev ^ hop) for dev in range(8)])  76.3 us
    all_gather x3, blocking collectives, on_device(): lax.all_gather(pressure, 'sub', axis=0, tiled=True)  49.1 us
    dot_general x3, matrix products, on_device(): jnp.einsum('jrc,jcl->jrl', leaf_inverse[0], rhs, precision=highest)  36.3 us
    all_gather x3, blocking collectives, on_device(): column = lax.all_gather(pressure, 'grp', axis=0, tiled=True)  29.8 us
    dot_general x3, matrix products, on_device(): jnp.einsum('jrs,sl->jrl', coupling[0], sep_value, precision=highest)  21.5 us
    dot_general x3, matrix products, on_device(): jnp.einsum('jrs,jrl->sl', coupling[0], solution, precision=highest)  15.3 us
    all_to_all x3, starting transfers between devices, on_device(): lax.all_to_all(outgoing.reshape(parts, CAP, width, loads), 'sub', split_a...  13.8 us
    ppermute x9, starting transfers between devices, on_device(): lax.ppermute(summed, 'sub', [(dev, dev ^ hop) for dev in range(8)])  12.3 us
  transfers between devices with their start and end apart: 16, of which 7 were waited for; matrix products, arithmetic and copies ran while one was open for 23% of the time, Pallas kernels for 0%

profile of v1, /device:TPU:0, one launch (start us, length us, event | category | flops | bytes accessed | tf_op | source)
XLA Modules:
  0.0 348.9 jit_solution(17141770843342330073)
XLA Ops:
  7.3 10.9 %all_gather.23 = f32[512,128]{1,0:T(8,128)S(1)} all-gather(f32[128,128]{1,0:T(8,128)} %param.20), channel_id=1, replica_groups=mesh['grp'=4,'sub'=8] {'grp'}, dimensions={0}, use_global_device_ids=true | all-gather | bytes 327680 | tf_op jit(solution)/shard_map/all_gather | solution.py:61
  18.1 2.6 fusion.130
  20.8 15.6 %all_gather.21 = f32[1024,128]{1,0:T(8,128)S(1)} all-gather(f32[128,128]{1,0:T(8,128)} %param.20), channel_id=1, replica_groups=mesh['grp'=4,'sub'=8] {'sub'}, dimensions={0}, use_global_device_ids=true | all-gather | bytes 589824 | tf_op jit(solution)/shard_map/all_gather | solution.py:72
  41.0 1.6 copy.77
  42.6 7.1 %fusion.51 = f32[2,1024,128]{1,2,0:T(8,128)S(1)} fusion(f32[2,1024,128]{1,2,0:T(8,128)} %copy.82, f32[1,2,1024,512]{3,2,1,0:T(8,128)} %param.15, f32[1,2,1024,128]{2,3,1,0:T(8,128)S(1)} %copy.77, f32[2,1024]{1,0:T(2,128)S(1)} %compare_convert_fusion), kind=kOutput, calls=%fused_computation.29 | convolution fusion | flops 1611399168 | bytes 7348224 | tf_op jit(solution)/shard_map/jrs,sl->jrl/dot_general | solution.py:77
  49.8 12.1 %fusion.57 = f32[2,1024,128]{1,2,0:T(8,128)} fusion(f32[2,1024,128]{1,2,0:T(8,128)S(1)} %fusion.51, f32[1,2,1024,1024]{3,2,1,0:T(8,128)} %param.14, f32[2,1024]{1,0:T(2,128)S(1)} %compare_convert_fusion), kind=kOutput, calls=%fused_computation.34 | convolution fusion | flops 3221487616 | bytes 10493952 | tf_op jit(solution)/shard_map/jrc,jcl->jrl/dot_general | solution.py:79
  64.9 2.4 fusion.85
  68.6 5.4 %all-to-all-start = ((f32[8,2,128,128]{3,2,1,0:T(8,128)}), f32[8,2,128,128]{3,2,1,0:T(8,128)}, u32[]{:S(2)}, u32[]{:S(2)}) async-start(f32[8,2,128,128]{3,2,1,0:T(8,128)} %copy.85), calls=%async_computation.1 | async-start | bytes 2097152 | tf_op jit(solution)/shard_map/all_to_all | solution.py:94
  74.7 4.9 %fusion.69 = f32[512,128]{0,1:T(8,128)S(1)} fusion(f32[2,1024,128]{1,2,0:T(8,128)} %fusion.57, f32[1,2,1024,512]{3,2,1,0:T(8,128)} %param.15), kind=kOutput, calls=%fused_computation.40 | convolution fusion | flops 1610612736 | bytes 5505024 | tf_op jit(solution)/shard_map/jrs,jrl->sl/dot_general | solution.py:80
  82.1 1.9 collective-permute-start.1
  85.1 20.8 %collective-permute-done.1 = f32[512,128]{0,1:T(8,128)} collective-permute-done((f32[512,128]{0,1:T(8,128)}, f32[512,128]{0,1:T(8,128)}, u32[]{:S(2)}, u32[]{:S(2)}) %collective-permute-start.1) | collective-permute-done | bytes 262176 | tf_op jit(solution)/shard_map/ppermute | solution.py:83
  105.9 1.8 add.68
  107.7 4.6 %collective-permute-start.2 = (f32[512,128]{0,1:T(8,128)}, f32[512,128]{0,1:T(8,128)}, u32[]{:S(2)}, u32[]{:S(2)}) collective-permute-start(f32[512,128]{0,1:T(8,128)} %add.68), channel_id=1, source_target_pairs={{0,4},{1,5},{2,6},{3,7},{4,0},{5,1},{6,2},{7,3},{8,12},{9,13},{10,... | collective-permute-start | bytes 786440 | tf_op jit(solution)/shard_map/ppermute | solution.py:83
  112.3 1.9 reduce_sum.37
  115.2 18.9 %all_gather.24 = f32[1024,128]{1,0:T(8,128)S(1)} all-gather(f32[128,128]{1,0:T(8,128)S(1)} %add_add_fusion.2), channel_id=1, replica_groups=mesh['grp'=4,'sub'=8] {'sub'}, dimensions={0}, use_global_device_ids=true | all-gather | bytes 589824 | tf_op jit(solution)/shard_map/all_gather | solution.py:72
  134.1 1.8 convolution_multiply_fusion.1
  137.1 2.5 copy.88
  139.7 2.1 convolution_bitcast_fusion.3
  141.8 7.2 %fusion.42 = f32[2,1024,128]{1,2,0:T(8,128)S(1)} fusion(f32[2,1024,128]{1,2,0:T(8,128)} %copy.88, f32[128,512,1]{1,0,2:T(8,128)S(1)} %convolution_bitcast_fusion.3, f32[1,2,1024,512]{3,2,1,0:T(8,128)} %param.15, f32[1,2,1024,128]{2,3,1,0:T(8,128)} %copy-done.2, f32[2,1024]{1,0:T(2,128)S(1)} %compare_convert_fusion), kind=kOutput, calls=%fused_computation.26 | convolution fusion | flops 1611399168 | bytes 7610368 | tf_op jit(solution)/shard_map/jrs,sl->jrl/dot_general | solution.py:77
  149.0 12.1 %fusion.63 = f32[2,1024,128]{1,2,0:T(8,128)} fusion(f32[2,1024,128]{1,2,0:T(8,128)S(1)} %fusion.42, f32[1,2,1024,1024]{3,2,1,0:T(8,128)} %param.14, f32[2,1024]{1,0:T(2,128)S(1)} %compare_convert_fusion), kind=kOutput, calls=%fused_computation.36 | convolution fusion | flops 3221487616 | bytes 10493952 | tf_op jit(solution)/shard_map/jrc,jcl->jrl/dot_general | solution.py:79
  161.1 2.5 copy.90
  163.6 2.4 reshape.166
  166.0 2.5 fusion.83
  169.7 4.2 %all-to-all-start.1 = ((f32[8,2,128,128]{3,2,1,0:T(8,128)}), f32[8,2,128,128]{3,2,1,0:T(8,128)}, u32[]{:S(2)}, u32[]{:S(2)}) async-start(f32[8,2,128,128]{3,2,1,0:T(8,128)} %copy.92), calls=%async_computation.3 | async-start | bytes 2097152 | tf_op jit(solution)/shard_map/all_to_all | solution.py:94
  174.0 8.3 %all_gather.25 = f32[512,128]{1,0:T(8,128)S(1)} all-gather(f32[128,128]{1,0:T(8,128)S(1)} %add_add_fusion.2), channel_id=1, replica_groups=mesh['grp'=4,'sub'=8] {'grp'}, dimensions={0}, use_global_device_ids=true | all-gather | bytes 327680 | tf_op jit(solution)/shard_map/all_gather | solution.py:61
  182.2 3.1 convolution_bitcast_fusion.1
  185.4 5.0 %fusion.72 = f32[512,128]{0,1:T(8,128)S(1)} fusion(f32[2,1024,128]{1,2,0:T(8,128)} %fusion.63, f32[1,2,1024,512]{3,2,1,0:T(8,128)} %param.15), kind=kOutput, calls=%fused_computation.41 | convolution fusion | flops 1610612736 | bytes 5505024 | tf_op jit(solution)/shard_map/jrs,jrl->sl/dot_general | solution.py:80
  192.0 1.9 collective-permute-start.4
  194.0 13.0 %collective-permute-done.4 = f32[512,128]{0,1:T(8,128)S(1)} collective-permute-done((f32[512,128]{0,1:T(8,128)S(1)}, f32[512,128]{0,1:T(8,128)S(1)}, u32[]{:S(2)}, u32[]{:S(2)}) %collective-permute-start.4) | collective-permute-done | bytes 262176 | tf_op jit(solution)/shard_map/ppermute | solution.py:83
  209.3 13.9 %collective-permute-done.5 = f32[512,128]{0,1:T(8,128)} collective-permute-done((f32[512,128]{0,1:T(8,128)}, f32[512,128]{0,1:T(8,128)}, u32[]{:S(2)}, u32[]{:S(2)}) %collective-permute-start.5) | collective-permute-done | bytes 262176 | tf_op jit(solution)/shard_map/ppermute | solution.py:83
  223.2 2.8 convolution_bitcast_fusion.2
  229.0 14.6 %all_gather.26 = f32[1024,128]{0,1:T(8,128)S(1)} all-gather(f32[128,128]{0,1:T(8,128)S(1)} %add_add_fusion.1), channel_id=1, replica_groups=mesh['grp'=4,'sub'=8] {'sub'}, dimensions={0}, use_global_device_ids=true | all-gather | bytes 589824 | tf_op jit(solution)/shard_map/all_gather | solution.py:72
  244.5 2.1 copy.95
  246.6 2.1 convolution_multiply_fusion
  249.9 2.5 copy.97
  252.5 7.2 %fusion.33 = f32[2,1024,128]{1,2,0:T(8,128)S(1)} fusion(f32[2,1024,128]{1,2,0:T(8,128)} %copy.97, f32[128,512,1]{1,0,2:T(8,128)} %convolution_bitcast_fusion.2, f32[1,2,1024,512]{3,2,1,0:T(8,128)} %param.15, f32[1,2,1024,128]{2,3,1,0:T(8,128)} %copy-done.2, f32[2,1024]{1,0:T(2,128)S(1)} %compare_convert_fusion), kind=kOutput, calls=%fused_computation.23 | convolution fusion | flops 1611399168 | bytes 7610368 | tf_op jit(solution)/shard_map/jrs,sl->jrl/dot_general | solution.py:77
  259.7 12.1 %fusion.66 = f32[2,128,1024]{2,1,0:T(8,128)} fusion(f32[2,1024,128]{1,2,0:T(8,128)S(1)} %fusion.33, f32[1,2,1024,1024]{3,2,1,0:T(8,128)} %param.14, f32[2,1024]{1,0:T(2,128)S(1)} %compare_convert_fusion), kind=kOutput, calls=%fused_computation.37 | convolution fusion | flops 3221487616 | bytes 10493952 | tf_op jit(solution)/shard_map/jrc,jcl->jrl/dot_general | solution.py:79
  271.8 2.6 copy.99
  274.4 2.4 reshape.169
  276.8 2.4 fusion.81
  280.4 4.2 %all-to-all-start.2 = ((f32[8,2,128,128]{3,2,1,0:T(8,128)}), f32[8,2,128,128]{3,2,1,0:T(8,128)}, u32[]{:S(2)}, u32[]{:S(2)}) async-start(f32[8,2,128,128]{3,2,1,0:T(8,128)} %copy.101), calls=%async_computation.5 | async-start | bytes 2097152 | tf_op jit(solution)/shard_map/all_to_all | solution.py:94
  284.9 5.3 %fusion.75 = f32[512,128]{0,1:T(8,128)} fusion(f32[1,2,1024,512]{3,2,1,0:T(8,128)} %param.15, f32[2,128,1024]{2,1,0:T(8,128)S(1)} %copy-done.1), kind=kOutput, calls=%fused_computation.42 | convolution fusion | flops 1610612736 | bytes 5505024 | tf_op jit(solution)/shard_map/jrs,jrl->sl/dot_general | solution.py:80
  290.6 10.7 %all_gather.27 = f32[512,128]{0,1:T(8,128)S(1)} all-gather(f32[128,128]{0,1:T(8,128)S(1)} %add_add_fusion.1), channel_id=1, replica_groups=mesh['grp'=4,'sub'=8] {'grp'}, dimensions={0}, use_global_device_ids=true | all-gather | bytes 327680 | tf_op jit(solution)/shard_map/all_gather | solution.py:61
  301.2 3.1 convolution_bitcast_fusion
  305.4 2.0 collective-permute-start.7
  307.5 10.5 %collective-permute-done.7 = f32[512,128]{0,1:T(8,128)S(1)} collective-permute-done((f32[512,128]{0,1:T(8,128)S(1)}, f32[512,128]{0,1:T(8,128)S(1)}, u32[]{:S(2)}, u32[]{:S(2)}) %collective-permute-start.7) | collective-permute-done | bytes 262176 | tf_op jit(solution)/shard_map/ppermute | solution.py:83
  320.0 15.3 %collective-permute-done.8 = f32[512,128]{0,1:T(8,128)} collective-permute-done((f32[512,128]{0,1:T(8,128)}, f32[512,128]{0,1:T(8,128)}, u32[]{:S(2)}, u32[]{:S(2)}) %collective-permute-start.8) | collective-permute-done | bytes 262176 | tf_op jit(solution)/shard_map/ppermute | solution.py:83
  335.3 3.2 fusion.87
  (90 shorter events, 34.3 us)
Async XLA Ops:
  7.2 11.0 %copy-start = (f32[1024,512]{1,0:T(8,128)S(1)}, f32[1024,512]{1,0:T(8,128)}, u32[]{:S(2)}) copy-start(f32[1024,512]{1,0:T(8,128)} %param.13) | copy-start | bytes 6291460
  7.2 29.7 %copy-start.10 = (s32[1,2,8,1]{2,3,1,0:T(1,128)S(1)}, s32[1,2,8,1]{2,3,1,0:T(1,128)}, u32[]{:S(2)}) copy-start(s32[1,2,8,1]{2,3,1,0:T(1,128)} %param.25) | copy-start | bytes 196
  7.2 30.4 %copy-start.12 = (s32[1,2]{1,0:T(1,128)S(1)}, s32[1,2]{1,0:T(1,128)}, u32[]{:S(2)}) copy-start(s32[1,2]{1,0:T(1,128)} %param.24) | copy-start | bytes 28
  7.2 30.6 %copy-start.5 = (f32[1,2,8,128]{3,2,1,0:T(8,128)S(1)}, f32[1,2,8,128]{3,2,1,0:T(8,128)}, u32[]{:S(2)}) copy-start(f32[1,2,8,128]{3,2,1,0:T(8,128)} %param.21) | copy-start | bytes 24580
  7.2 107.0 %reduce-scatter.4.cloned.1.call-start = ((), (), s32[]{:S(2)}) async-start(), calls=%async_computation.6 | async-start | bytes 589824 | tf_op jit(solution)/shard_map/reduce_scatter | solution.py:66
  20.7 20.1 %copy-start.11 = (s32[1,2]{1,0:T(1,128)S(1)}, s32[1,2]{1,0:T(1,128)}, u32[]{:S(2)}) copy-start(s32[1,2]{1,0:T(1,128)} %param.23) | copy-start | bytes 28
  20.8 21.8 %copy-start.6 = (f32[1,2,8,128]{3,2,1,0:T(8,128)S(1)}, f32[1,2,8,128]{3,2,1,0:T(8,128)}, u32[]{:S(2)}) copy-start(f32[1,2,8,128]{3,2,1,0:T(8,128)} %param.22) | copy-start | bytes 24580
  37.6 12.2 %copy-start.9 = (s32[16]{0:T(128)}, s32[16]{0:T(128)S(1)}, u32[]{:S(2)}) copy-start(s32[16]{0:T(128)S(1)} %eq.58) | copy-start | bytes 196
  42.5 19.4 %copy-start.2 = (f32[1,2,1024,128]{2,3,1,0:T(8,128)}, f32[1,2,1024,128]{2,3,1,0:T(8,128)S(1)}, u32[]{:S(2)}) copy-start(f32[1,2,1024,128]{2,3,1,0:T(8,128)S(1)} %copy.77) | copy-start | bytes 3145732
  42.5 22.4 %copy-start.7 = (s32[16]{0:T(128)}, s32[16]{0:T(128)S(1)}, u32[]{:S(2)}) copy-start(s32[16]{0:T(128)S(1)} %multiply_add_fusion.1) | copy-start | bytes 196
  68.6 43.7 %all-to-all-start = ((f32[8,2,128,128]{3,2,1,0:T(8,128)}), f32[8,2,128,128]{3,2,1,0:T(8,128)}, u32[]{:S(2)}, u32[]{:S(2)}) async-start(f32[8,2,128,128]{3,2,1,0:T(8,128)} %copy.85), calls=%async_computation.1 | async-start | bytes 2097152 | tf_op jit(solution)/shard_map/all_to_all | solution.py:94
  73.9 65.7 %all-gather.3.cloned.1.call-start = ((), (), s32[]{:S(2)}) async-start(), calls=%async_computation.9 | async-start | bytes 1179648 | tf_op jit(solution)/shard_map/all_gather | solution.py:56
  79.7 1.7 collective-permute-start
  82.1 23.8 %collective-permute-start.1 = (f32[512,128]{0,1:T(8,128)}, f32[512,128]{0,1:T(8,128)}, u32[]{:S(2)}, u32[]{:S(2)}) collective-permute-start(f32[512,128]{0,1:T(8,128)} %add.67), channel_id=1, source_target_pairs={{0,2},{1,3},{2,0},{3,1},{4,6},{5,7},{6,4},{7,5},{8,10},{9,11},{10,... | collective-permute-start | bytes 786440 | tf_op jit(solution)/shard_map/ppermute | solution.py:83
  107.7 32.0 %collective-permute-start.2 = (f32[512,128]{0,1:T(8,128)}, f32[512,128]{0,1:T(8,128)}, u32[]{:S(2)}, u32[]{:S(2)}) collective-permute-start(f32[512,128]{0,1:T(8,128)} %add.68), channel_id=1, source_target_pairs={{0,4},{1,5},{2,6},{3,7},{4,0},{5,1},{6,2},{7,3},{8,12},{9,13},{10,... | collective-permute-start | bytes 786440 | tf_op jit(solution)/shard_map/ppermute | solution.py:83
  169.7 56.4 %all-to-all-start.1 = ((f32[8,2,128,128]{3,2,1,0:T(8,128)}), f32[8,2,128,128]{3,2,1,0:T(8,128)}, u32[]{:S(2)}, u32[]{:S(2)}) async-start(f32[8,2,128,128]{3,2,1,0:T(8,128)} %copy.92), calls=%async_computation.3 | async-start | bytes 2097152 | tf_op jit(solution)/shard_map/all_to_all | solution.py:94
  173.9 54.1 %reduce-scatter.6.cloned.1.call-start = ((), (), s32[]{:S(2)}) async-start(), calls=%async_computation.7 | async-start | bytes 589824 | tf_op jit(solution)/shard_map/reduce_scatter | solution.py:66
  185.4 23.2 %copy-start.4 = (f32[128,128]{1,0:T(8,128)S(1)}, f32[128,128]{1,0:T(8,128)}, u32[]{:S(2)}) copy-start(f32[128,128]{1,0:T(8,128)} %param.19) | copy-start | bytes 196612
  190.4 1.6 collective-permute-start.3
  192.0 15.0 %collective-permute-start.4 = (f32[512,128]{0,1:T(8,128)S(1)}, f32[512,128]{0,1:T(8,128)S(1)}, u32[]{:S(2)}, u32[]{:S(2)}) collective-permute-start(f32[512,128]{0,1:T(8,128)S(1)} %add.73), channel_id=1, source_target_pairs={{0,2},{1,3},{2,0},{3,1},{4,6},{5,7},{6,4},{7,5},{8,10},{9,11},{10,... | collective-permute-start | bytes 786440 | tf_op jit(solution)/shard_map/ppermute | solution.py:83
  207.8 15.4 %collective-permute-start.5 = (f32[512,128]{0,1:T(8,128)}, f32[512,128]{0,1:T(8,128)}, u32[]{:S(2)}, u32[]{:S(2)}) collective-permute-start(f32[512,128]{0,1:T(8,128)} %add.74), channel_id=1, source_target_pairs={{0,4},{1,5},{2,6},{3,7},{4,0},{5,1},{6,2},{7,3},{8,12},{9,13},{10,... | collective-permute-start | bytes 786440 | tf_op jit(solution)/shard_map/ppermute | solution.py:83
  271.8 4.9 %copy-start.8 = (s32[16]{0:T(128)S(1)}, s32[16]{0:T(128)}, u32[]{:S(2)}) copy-start(s32[16]{0:T(128)} %copy-done.7) | copy-start | bytes 196
  279.2 5.7 %copy-start.1 = (f32[2,128,1024]{2,1,0:T(8,128)S(1)}, f32[2,128,1024]{2,1,0:T(8,128)}, u32[]{:S(2)}) copy-start(f32[2,128,1024]{2,1,0:T(8,128)} %fusion.66) | copy-start | bytes 3145732
  280.4 58.8 %all-to-all-start.2 = ((f32[8,2,128,128]{3,2,1,0:T(8,128)}), f32[8,2,128,128]{3,2,1,0:T(8,128)}, u32[]{:S(2)}, u32[]{:S(2)}) async-start(f32[8,2,128,128]{3,2,1,0:T(8,128)} %copy.101), calls=%async_computation.5 | async-start | bytes 2097152 | tf_op jit(solution)/shard_map/all_to_all | solution.py:94
  284.6 55.9 %reduce-scatter.8.cloned.1.call-start = ((), (), s32[]{:S(2)}) async-start(), calls=%async_computation.8 | async-start | bytes 589824 | tf_op jit(solution)/shard_map/reduce_scatter | solution.py:66
  290.2 14.1 %collective-permute-start.6 = (f32[512,128]{0,1:T(8,128)}, f32[512,128]{0,1:T(8,128)}, u32[]{:S(2)}, u32[]{:S(2)}) collective-permute-start(f32[512,128]{0,1:T(8,128)} %fusion.75), channel_id=1, source_target_pairs={{0,1},{1,0},{2,3},{3,2},{4,5},{5,4},{6,7},{7,6},{8,9},{9,8},{10,11... | collective-permute-start | bytes 786440 | tf_op jit(solution)/shard_map/ppermute | solution.py:83
  304.3 36.3 %copy-start.3 = (f32[128,128]{0,1:T(8,128)S(1)}, f32[128,128]{0,1:T(8,128)}, u32[]{:S(2)}) copy-start(f32[128,128]{0,1:T(8,128)} %copy.89) | copy-start | bytes 196612
  305.4 12.6 %collective-permute-start.7 = (f32[512,128]{0,1:T(8,128)S(1)}, f32[512,128]{0,1:T(8,128)S(1)}, u32[]{:S(2)}, u32[]{:S(2)}) collective-permute-start(f32[512,128]{0,1:T(8,128)S(1)} %add.78), channel_id=1, source_target_pairs={{0,2},{1,3},{2,0},{3,1},{4,6},{5,7},{6,4},{7,5},{8,10},{9,11},{10,... | collective-permute-start | bytes 786440 | tf_op jit(solution)/shard_map/ppermute | solution.py:83
  318.7 16.6 %collective-permute-start.8 = (f32[512,128]{0,1:T(8,128)}, f32[512,128]{0,1:T(8,128)}, u32[]{:S(2)}, u32[]{:S(2)}) collective-permute-start(f32[512,128]{0,1:T(8,128)} %add.79), channel_id=1, source_target_pairs={{0,4},{1,5},{2,6},{3,7},{4,0},{5,1},{6,2},{7,3},{8,12},{9,13},{10,... | collective-permute-start | bytes 786440 | tf_op jit(solution)/shard_map/ppermute | solution.py:83
Sparse Core Ops, SparseCore 0:
  20.9 31.6 reduce-scatter.3
  76.4 32.4 all-gather.2
  185.5 32.6 reduce-scatter.5
  304.5 32.2 reduce-scatter.7
